TPU v7x, 256 devices: a whole 4x4x8 slice. The times are simulated.
256 devices in a mesh: ctx: 64 (over z, y, core), kvh: 4 (over x).
Axes of the slice: x: 4, y: 4, z: 8, core: 2. Of those that a mesh axis runs over, the one named last changes fastest.
Arguments:
- queries: bfloat16 [32768, 3584], P('ctx', 'kvh'), may hold values from -384 to 384
- key_block: bfloat16 [32768, 512], P('ctx', 'kvh'), may hold values from -8 to 8
- value_block: bfloat16 [32768, 512], P('ctx', 'kvh'), may hold values from -6 to 6
- block_valid: int32 [64], replicated, may hold values from 2 to 512, as said below
- out_weight: bfloat16 [3584, 3584], P('kvh'), may hold values from -6 to 6
Outputs:
- projected: bfloat16 [32768, 3584], P(('ctx', 'kvh'))
Inputs may be any that keep to these rules, and one draw needn't show every extreme that they name: `block_valid`: every entry but the last equals 512.
All inputs are finite; a program needn't handle non-finite values.
Results may differ from a plain program's by a relative error of at most 0.01.
Values may be sent and summed in bfloat16 or wider, within the bound.
A program may use at most 128 MiB of HBM per device.

v0:
```python
import jax
import jax.numpy as jnp
from jax import lax
from jax.sharding import PartitionSpec as P


def passed_along(block, axis, distance):
    devices = range(lax.axis_size(axis))
    route = [(i - distance, i) for i in devices if i - distance in devices]
    return lax.ppermute(block, axis, route)


def split_up(x, dim, length):
    shape = x.shape
    tiles = x.reshape(*shape[:dim], length, shape[dim] // length, *shape[dim + 1 :])
    return jnp.moveaxis(tiles, dim, 0)


def sum_at_owner(x, axis, dim):
    length = lax.axis_size(axis)
    tiles = lax.all_to_all(split_up(x, dim, length), axis, 0, 0, tiled=True)
    return jnp.sum(tiles.astype(jnp.float32), axis=0)


def per_device(queries, key_block, value_block, block_valid, out_weight):
    row_count = queries.shape[0]
    head_size = key_block.shape[1]
    group_size = queries.shape[1] // head_size
    ctx_size = lax.axis_size("ctx")
    block_id = lax.axis_index("ctx")
    offsets = [1 << level_id for level_id in range((ctx_size - 1).bit_length())]
    position = jnp.arange(row_count, dtype=jnp.int32)
    key_list = [key_block]
    value_list = [value_block]
    mask_list = [
        (position[None, :] <= position[:, None]) & (position[None, :] < block_valid[block_id])
    ]
    for offset in offsets:
        moved_keys, moved_values = passed_along((key_block, value_block), "ctx", offset)
        key_list.append(moved_keys)
        value_list.append(moved_values)
    for offset in offsets:
        source = jnp.maximum(block_id - offset, 0)
        usable = (block_id - offset >= 0) & (position < block_valid[source])
        mask_list.append(jnp.broadcast_to(usable[None, :], (row_count, row_count)))
    keys_cat = jnp.concatenate(key_list, axis=0)
    values_cat = jnp.concatenate(value_list, axis=0)
    allowed = jnp.concatenate(mask_list, axis=1)
    query_heads = queries.reshape(row_count, group_size, head_size)
    score_scale = head_size ** (-0.5)
    results = []
    for head_id in range(group_size):
        scores = (
            lax.dot_general(
                query_heads[:, head_id, :],
                keys_cat,
                (((1,), (1,)), ((), ())),
                preferred_element_type=jnp.float32,
            )
            * score_scale
        )
        scores = jnp.where(allowed, scores, -1e30)
        row_max = jnp.max(scores, axis=-1, keepdims=True)
        numerators = jnp.where(allowed, jnp.exp(scores - row_max), 0.0)
        row_total = jnp.sum(numerators, axis=-1)
        weights = numerators.astype(jnp.bfloat16)
        mixture = (
            jnp.dot(weights, values_cat, preferred_element_type=jnp.float32) / row_total[:, None]
        )
        results.append(mixture.astype(jnp.bfloat16))
    attended = jnp.concatenate(results, axis=1)
    summed = sum_at_owner(
        jnp.dot(attended, out_weight, preferred_element_type=jnp.float32).astype(jnp.bfloat16),
        "kvh",
        0,
    )
    return summed.astype(jnp.bfloat16)


def solution(mesh):
    return jax.shard_map(
        per_device,
        mesh=mesh,
        in_specs=(P("ctx", "kvh"), P("ctx", "kvh"), P("ctx", "kvh"), P(), P("kvh", None)),
        out_specs=P(("ctx", "kvh"), None),
        check_vma=False,
    )
```

profile of v0, /device:TPU:8, one launch (start us, length us, event | category | flops | bytes accessed | tf_op | source)
XLA Modules:
  0.0 185.2 jit_solution(14166663071464561966)
XLA Ops:
  0.0 1.9 %collective-permute-start = (bf16[512,128]{1,0:T(8,128)(2,1)}, bf16[512,128]{1,0:T(8,128)(2,1)S(1)}, u32[]{:S(2)}, u32[]{:S(2)}) collective-permute-start(bf16[512,128]{1,0:T(8,128)(2,1)} %param.6), channel_id=1, source_target_pairs={{0,4},{4,8},{8,12},{12,16},{16,20},{20,24},{24,28},{28,32},{32,36}... | collective-permute-start | bytes 393224 | tf_op jit(solution)/shard_map/ppermute | solution.py:10
  1.9 3.5 %collective-permute-start.1 = (bf16[512,128]{1,0:T(8,128)(2,1)}, bf16[512,128]{1,0:T(8,128)(2,1)S(1)}, u32[]{:S(2)}, u32[]{:S(2)}) collective-permute-start(bf16[512,128]{1,0:T(8,128)(2,1)} %param.6), channel_id=1, source_target_pairs={{0,8},{4,12},{8,16},{12,20},{16,24},{20,28},{24,32},{28,36},{32,40... | collective-permute-start | bytes 393224 | tf_op jit(solution)/shard_map/ppermute | solution.py:10
  5.4 4.2 %collective-permute-start.2 = (bf16[512,128]{1,0:T(8,128)(2,1)}, bf16[512,128]{1,0:T(8,128)(2,1)S(1)}, u32[]{:S(2)}, u32[]{:S(2)}) collective-permute-start(bf16[512,128]{1,0:T(8,128)(2,1)} %param.6), channel_id=1, source_target_pairs={{0,16},{4,20},{8,24},{12,28},{16,32},{20,36},{24,40},{28,44},{32,4... | collective-permute-start | bytes 393224 | tf_op jit(solution)/shard_map/ppermute | solution.py:10
  9.6 3.8 %collective-permute-start.3 = (bf16[512,128]{1,0:T(8,128)(2,1)}, bf16[512,128]{1,0:T(8,128)(2,1)S(1)}, u32[]{:S(2)}, u32[]{:S(2)}) collective-permute-start(bf16[512,128]{1,0:T(8,128)(2,1)} %param.6), channel_id=1, source_target_pairs={{0,32},{4,36},{8,40},{12,44},{16,48},{20,52},{24,56},{28,60},{32,6... | collective-permute-start | bytes 393224 | tf_op jit(solution)/shard_map/ppermute | solution.py:10
  13.5 6.4 %collective-permute-start.4 = (bf16[512,128]{1,0:T(8,128)(2,1)}, bf16[512,128]{1,0:T(8,128)(2,1)S(1)}, u32[]{:S(2)}, u32[]{:S(2)}) collective-permute-start(bf16[512,128]{1,0:T(8,128)(2,1)} %param.6), channel_id=1, source_target_pairs={{0,64},{4,68},{8,72},{12,76},{16,80},{20,84},{24,88},{28,92},{32,9... | collective-permute-start | bytes 393224 | tf_op jit(solution)/shard_map/ppermute | solution.py:10
  19.9 1.6 fusion.120
  27.3 1.6 constant_dynamic-update-slice_fusion.6
  28.8 1.6 constant_dynamic-update-slice_fusion.13
  31.9 3.3 %collective-permute-start.5 = (bf16[512,128]{1,0:T(8,128)(2,1)}, bf16[512,128]{1,0:T(8,128)(2,1)S(1)}, u32[]{:S(2)}, u32[]{:S(2)}) collective-permute-start(bf16[512,128]{1,0:T(8,128)(2,1)} %param.6), channel_id=1, source_target_pairs={{0,128},{4,132},{8,136},{12,140},{16,144},{20,148},{24,152},{28,15... | collective-permute-start | bytes 393224 | tf_op jit(solution)/shard_map/ppermute | solution.py:10
  35.8 2.5 %collective-permute-start.6 = (bf16[512,128]{1,0:T(8,128)(2,1)}, bf16[512,128]{1,0:T(8,128)(2,1)S(1)}, u32[]{:S(2)}, u32[]{:S(2)}) collective-permute-start(bf16[512,128]{1,0:T(8,128)(2,1)} %param.7), channel_id=1, source_target_pairs={{0,4},{4,8},{8,12},{12,16},{16,20},{20,24},{24,28},{28,32},{32,36}... | collective-permute-start | bytes 393224 | tf_op jit(solution)/shard_map/ppermute | solution.py:10
  39.0 2.9 %collective-permute-start.7 = (bf16[512,128]{1,0:T(8,128)(2,1)}, bf16[512,128]{1,0:T(8,128)(2,1)S(1)}, u32[]{:S(2)}, u32[]{:S(2)}) collective-permute-start(bf16[512,128]{1,0:T(8,128)(2,1)} %param.7), channel_id=1, source_target_pairs={{0,8},{4,12},{8,16},{12,20},{16,24},{20,28},{24,32},{28,36},{32,40... | collective-permute-start | bytes 393224 | tf_op jit(solution)/shard_map/ppermute | solution.py:10
  42.5 4.4 %collective-permute-start.8 = (bf16[512,128]{1,0:T(8,128)(2,1)}, bf16[512,128]{1,0:T(8,128)(2,1)S(1)}, u32[]{:S(2)}, u32[]{:S(2)}) collective-permute-start(bf16[512,128]{1,0:T(8,128)(2,1)} %param.7), channel_id=1, source_target_pairs={{0,16},{4,20},{8,24},{12,28},{16,32},{20,36},{24,40},{28,44},{32,4... | collective-permute-start | bytes 393224 | tf_op jit(solution)/shard_map/ppermute | solution.py:10
  47.6 2.9 %collective-permute-start.9 = (bf16[512,128]{1,0:T(8,128)(2,1)}, bf16[512,128]{1,0:T(8,128)(2,1)}, u32[]{:S(2)}, u32[]{:S(2)}) collective-permute-start(bf16[512,128]{1,0:T(8,128)(2,1)} %param.7), channel_id=1, source_target_pairs={{0,32},{4,36},{8,40},{12,44},{16,48},{20,52},{24,56},{28,60},{32,6... | collective-permute-start | bytes 393224 | tf_op jit(solution)/shard_map/ppermute | solution.py:10
  51.2 2.5 %collective-permute-start.10 = (bf16[512,128]{1,0:T(8,128)(2,1)}, bf16[512,128]{1,0:T(8,128)(2,1)}, u32[]{:S(2)}, u32[]{:S(2)}) collective-permute-start(bf16[512,128]{1,0:T(8,128)(2,1)} %param.7), channel_id=1, source_target_pairs={{0,64},{4,68},{8,72},{12,76},{16,80},{20,84},{24,88},{28,92},{32,9... | collective-permute-start | bytes 393224 | tf_op jit(solution)/shard_map/ppermute | solution.py:10
  54.3 6.2 %fusion.121 = (f32[512]{0:T(512)}, f32[512,3584]{0,1:T(8,128)}) fusion(pred[512,3584]{0,1:T(8,128)(4,1)S(1)} %broadcast_dynamic-update-slice_fusion, bf16[3584,128]{1,0:T(8,128)(2,1)} %constant_dynamic-update-slice_fusion, bf16[512,7,128]{0,2,1:T(8,128)(2,1)S(1)} %bitcast.90), kind=kOutput, calls=%fused_computation.122 | convolution fusion | flops 475266560 | bytes 10225664 | tf_op jit(solution)/shard_map/dot_general | solution.py:54
  63.3 4.4 %fusion.124 = (f32[512]{0:T(512)S(1)}, f32[512,3584]{0,1:T(8,128)}) fusion(pred[512,3584]{0,1:T(8,128)(4,1)S(1)} %broadcast_dynamic-update-slice_fusion, bf16[3584,128]{1,0:T(8,128)(2,1)S(1)} %copy-done.2, bf16[512,7,128]{0,2,1:T(8,128)(2,1)S(1)} %bitcast.93), kind=kOutput, calls=%fused_computation.125 | convolution fusion | flops 475266560 | bytes 10225664 | tf_op jit(solution)/shard_map/dot_general | solution.py:54
  67.7 5.0 %fusion.125 = (f32[512]{0:T(512)}, f32[512,3584]{0,1:T(8,128)}) fusion(pred[512,3584]{0,1:T(8,128)(4,1)S(1)} %broadcast_dynamic-update-slice_fusion, bf16[3584,128]{1,0:T(8,128)(2,1)S(1)} %copy-done.2, bf16[512,7,128]{0,2,1:T(8,128)(2,1)S(1)} %bitcast.94), kind=kOutput, calls=%fused_computation.126 | convolution fusion | flops 475266560 | bytes 10225664 | tf_op jit(solution)/shard_map/dot_general | solution.py:54
  72.7 5.0 %fusion.126 = (f32[512]{0:T(512)}, f32[512,3584]{0,1:T(8,128)}) fusion(pred[512,3584]{0,1:T(8,128)(4,1)S(1)} %broadcast_dynamic-update-slice_fusion, bf16[3584,128]{1,0:T(8,128)(2,1)S(1)} %copy-done.2, bf16[512,7,128]{0,2,1:T(8,128)(2,1)S(1)} %bitcast.95), kind=kOutput, calls=%fused_computation.127 | convolution fusion | flops 475266560 | bytes 10225664 | tf_op jit(solution)/shard_map/dot_general | solution.py:54
  77.7 5.0 %fusion.127 = (f32[512]{0:T(512)}, f32[512,3584]{0,1:T(8,128)}) fusion(pred[512,3584]{0,1:T(8,128)(4,1)S(1)} %broadcast_dynamic-update-slice_fusion, bf16[3584,128]{1,0:T(8,128)(2,1)S(1)} %copy-done.2, bf16[512,7,128]{0,2,1:T(8,128)(2,1)S(1)} %bitcast.96), kind=kOutput, calls=%fused_computation.128 | convolution fusion | flops 475266560 | bytes 10225664 | tf_op jit(solution)/shard_map/dot_general | solution.py:54
  82.7 18.5 %fusion.12 = (f32[512]{0:T(512)S(1)}, f32[512]{0:T(512)S(1)}, f32[512]{0:T(512)S(1)}, f32[512]{0:T(512)S(1)}, f32[512]{0:T(512)S(1)}, /*index=5*/f32[512]{0:T(512)S(1)}, f32[512]{0:T(512)S(1)}) fusion(pred[512,3584]{0,1:T(8,128)(4,1)S(1)} %broadcast_dynamic-update-slice_fusion, f32[512,3584]{0,1:T(8,128)S(1)} %get-tuple-element.22, ...), kind=kLoop, calls=%fused_computation.27 | loop fusion | flops 38531584 | bytes 53243904 | tf_op jit(solution)/shard_map/reduce_sum | solution.py:65
  104.6 1.6 constant_dynamic-update-slice_fusion.9
  106.2 1.6 constant_dynamic-update-slice_fusion.8
  108.4 6.0 %fusion.48 = bf16[512,896]{1,0:T(8,128)(2,1)S(1)} fusion(bf16[3584,128]{1,0:T(8,128)(2,1)} %constant_dynamic-update-slice_fusion.7, pred[512,3584]{0,1:T(8,128)(4,1)S(1)} %broadcast_dynamic-update-slice_fusion, f32[512,3584]{0,1:T(8,128)} %get-tuple-element.20, f32[512]{0:T(512)S(1)} %copy-done.4, f32[512]{0:T(512)S(1)} %get-tuple-element.11), kind=kOutput, calls=%fused_computation.52 | convolution fusion | flops 475398144 | bytes 10227712 | tf_op jit(solution)/shard_map/dot_general | solution.py:68
  114.5 2.3 %fusion.57 = bf16[512,896]{1,0:T(8,128)(2,1)S(1)} fusion(bf16[512,896]{1,0:T(8,128)(2,1)S(1)} %fusion.48, bf16[3584,128]{1,0:T(8,128)(2,1)S(1)} %copy-done.1, pred[512,3584]{0,1:T(8,128)(4,1)S(1)} %broadcast_dynamic-update-slice_fusion, f32[512,3584]{0,1:T(8,128)S(1)} %bitcast.88, f32[512]{0:T(512)S(1)} %copy-done.6, f32[512]{0:T(512)S(1)} %get-tuple-element.10), kind=kOutput, calls=%fused_computation.55 | convolution fusion | flops 475398144 | bytes 10227712 | tf_op jit(solution)/shard_map/dot_general | solution.py:68
  117.6 2.3 %fusion.66 = bf16[512,896]{1,0:T(8,128)(2,1)S(1)} fusion(bf16[512,896]{1,0:T(8,128)(2,1)S(1)} %fusion.57, bf16[3584,128]{1,0:T(8,128)(2,1)S(1)} %copy-done.1, pred[512,3584]{0,1:T(8,128)(4,1)S(1)} %broadcast_dynamic-update-slice_fusion, f32[512,3584]{0,1:T(8,128)S(1)} %bitcast.86, f32[512]{0:T(512)S(1)} %copy-done.5, f32[512]{0:T(512)S(1)} %get-tuple-element.9), kind=kOutput, calls=%fused_computation.58 | convolution fusion | flops 475398144 | bytes 10227712 | tf_op jit(solution)/shard_map/dot_general | solution.py:68
  120.0 2.3 %fusion.75 = bf16[512,896]{1,0:T(8,128)(2,1)S(1)} fusion(bf16[512,896]{1,0:T(8,128)(2,1)S(1)} %fusion.66, bf16[3584,128]{1,0:T(8,128)(2,1)S(1)} %copy-done.1, pred[512,3584]{0,1:T(8,128)(4,1)S(1)} %broadcast_dynamic-update-slice_fusion, f32[512,3584]{0,1:T(8,128)S(1)} %bitcast.84, f32[512]{0:T(512)S(1)} %copy-done.3, f32[512]{0:T(512)S(1)} %get-tuple-element.8), kind=kOutput, calls=%fused_computation.61 | convolution fusion | flops 475398144 | bytes 10227712 | tf_op jit(solution)/shard_map/dot_general | solution.py:68
  123.0 2.3 %fusion.84 = bf16[512,896]{1,0:T(8,128)(2,1)S(1)} fusion(bf16[512,896]{1,0:T(8,128)(2,1)S(1)} %fusion.75, bf16[3584,128]{1,0:T(8,128)(2,1)S(1)} %copy-done.1, pred[512,3584]{0,1:T(8,128)(4,1)S(1)} %broadcast_dynamic-update-slice_fusion, f32[512,3584]{0,1:T(8,128)S(1)} %bitcast.82, f32[512]{0:T(512)S(1)} %get-tuple-element.25, f32[512]{0:T(512)S(1)} %get-tuple-element.7), kind=kOutput, calls=%fused_computation.64 | convolution fusion | flops 475398144 | bytes 10227712 | tf_op jit(solution)/shard_map/dot_general | solution.py:68
  125.3 2.3 %fusion.93 = bf16[512,896]{1,0:T(8,128)(2,1)S(1)} fusion(bf16[512,896]{1,0:T(8,128)(2,1)S(1)} %fusion.84, bf16[3584,128]{1,0:T(8,128)(2,1)S(1)} %copy-done.1, pred[512,3584]{0,1:T(8,128)(4,1)S(1)} %broadcast_dynamic-update-slice_fusion, f32[512,3584]{0,1:T(8,128)S(1)} %get-tuple-element.24, f32[512]{0:T(512)S(1)} %get-tuple-element.23, ...), kind=kOutput, calls=%fused_computation.67 | convolution fusion | flops 475398144 | bytes 10227712 | tf_op jit(solution)/shard_map/dot_general | solution.py:68
  127.6 2.5 %fusion.102 = bf16[512,896]{1,0:T(8,128)(2,1)S(1)} fusion(bf16[512,896]{1,0:T(8,128)(2,1)S(1)} %fusion.93, bf16[3584,128]{1,0:T(8,128)(2,1)S(1)} %copy-done.1, pred[512,3584]{0,1:T(8,128)(4,1)S(1)} %broadcast_dynamic-update-slice_fusion, f32[512,3584]{0,1:T(8,128)S(1)} %get-tuple-element.22, f32[512]{0:T(512)S(1)} %get-tuple-element.21, ...), kind=kOutput, calls=%fused_computation.70 | convolution fusion | flops 475398144 | bytes 10227712 | tf_op jit(solution)/shard_map/dot_general | solution.py:68
  130.5 4.2 %convolution_convert_fusion = bf16[512,3584]{1,0:T(8,128)(2,1)S(1)} fusion(bf16[512,896]{1,0:T(8,128)(2,1)S(1)} %fusion.102, bf16[896,3584]{1,0:T(8,128)(2,1)S(1)} %bitcast.98), kind=kOutput, calls=%fused_computation.14 | convolution fusion | flops 3290169344 | bytes 11010048 | tf_op jit(solution)/shard_map/dot_general | solution.py:73
  134.7 46.8 %all_to_all.5 = bf16[4,128,3584]{2,1,0:T(8,128)(2,1)} all-to-all(bf16[4,128,3584]{2,1,0:T(8,128)(2,1)S(1)} %bitcast.89), channel_id=1, replica_groups=mesh['ctx'=64,'kvh'=4] {'kvh'}, dimensions={0} | all-to-all | bytes 7340032 | tf_op jit(solution)/shard_map/all_to_all | solution.py:21
  181.5 3.8 %reduce_sum.82 = bf16[128,3584]{1,0:T(8,128)(2,1)} reduce(bf16[4,128,3584]{2,1,0:T(8,128)(2,1)} %all_to_all.5, bf16[]{:T(256)} %constant.43.clone.1), dimensions={0}, to_apply=%region_14.15 | reduce | flops 1376256 | bytes 4587522 | tf_op jit(solution)/shard_map/reduce_sum | solution.py:22
  (79 shorter events, 19.9 us)
Async XLA Ops:
  0.0 31.9 %collective-permute-start = (bf16[512,128]{1,0:T(8,128)(2,1)}, bf16[512,128]{1,0:T(8,128)(2,1)S(1)}, u32[]{:S(2)}, u32[]{:S(2)}) collective-permute-start(bf16[512,128]{1,0:T(8,128)(2,1)} %param.6), channel_id=1, source_target_pairs={{0,4},{4,8},{8,12},{12,16},{16,20},{20,24},{24,28},{28,32},{32,36}... | collective-permute-start | bytes 393224 | tf_op jit(solution)/shard_map/ppermute | solution.py:10
  1.9 33.9 %collective-permute-start.1 = (bf16[512,128]{1,0:T(8,128)(2,1)}, bf16[512,128]{1,0:T(8,128)(2,1)S(1)}, u32[]{:S(2)}, u32[]{:S(2)}) collective-permute-start(bf16[512,128]{1,0:T(8,128)(2,1)} %param.6), channel_id=1, source_target_pairs={{0,8},{4,12},{8,16},{12,20},{16,24},{20,28},{24,32},{28,36},{32,40... | collective-permute-start | bytes 393224 | tf_op jit(solution)/shard_map/ppermute | solution.py:10
  5.4 33.5 %collective-permute-start.2 = (bf16[512,128]{1,0:T(8,128)(2,1)}, bf16[512,128]{1,0:T(8,128)(2,1)S(1)}, u32[]{:S(2)}, u32[]{:S(2)}) collective-permute-start(bf16[512,128]{1,0:T(8,128)(2,1)} %param.6), channel_id=1, source_target_pairs={{0,16},{4,20},{8,24},{12,28},{16,32},{20,36},{24,40},{28,44},{32,4... | collective-permute-start | bytes 393224 | tf_op jit(solution)/shard_map/ppermute | solution.py:10
  9.6 32.9 %collective-permute-start.3 = (bf16[512,128]{1,0:T(8,128)(2,1)}, bf16[512,128]{1,0:T(8,128)(2,1)S(1)}, u32[]{:S(2)}, u32[]{:S(2)}) collective-permute-start(bf16[512,128]{1,0:T(8,128)(2,1)} %param.6), channel_id=1, source_target_pairs={{0,32},{4,36},{8,40},{12,44},{16,48},{20,52},{24,56},{28,60},{32,6... | collective-permute-start | bytes 393224 | tf_op jit(solution)/shard_map/ppermute | solution.py:10
  13.5 34.1 %collective-permute-start.4 = (bf16[512,128]{1,0:T(8,128)(2,1)}, bf16[512,128]{1,0:T(8,128)(2,1)S(1)}, u32[]{:S(2)}, u32[]{:S(2)}) collective-permute-start(bf16[512,128]{1,0:T(8,128)(2,1)} %param.6), channel_id=1, source_target_pairs={{0,64},{4,68},{8,72},{12,76},{16,80},{20,84},{24,88},{28,92},{32,9... | collective-permute-start | bytes 393224 | tf_op jit(solution)/shard_map/ppermute | solution.py:10
  31.9 19.3 %collective-permute-start.5 = (bf16[512,128]{1,0:T(8,128)(2,1)}, bf16[512,128]{1,0:T(8,128)(2,1)S(1)}, u32[]{:S(2)}, u32[]{:S(2)}) collective-permute-start(bf16[512,128]{1,0:T(8,128)(2,1)} %param.6), channel_id=1, source_target_pairs={{0,128},{4,132},{8,136},{12,140},{16,144},{20,148},{24,152},{28,15... | collective-permute-start | bytes 393224 | tf_op jit(solution)/shard_map/ppermute | solution.py:10
  35.8 65.4 %collective-permute-start.6 = (bf16[512,128]{1,0:T(8,128)(2,1)}, bf16[512,128]{1,0:T(8,128)(2,1)S(1)}, u32[]{:S(2)}, u32[]{:S(2)}) collective-permute-start(bf16[512,128]{1,0:T(8,128)(2,1)} %param.7), channel_id=1, source_target_pairs={{0,4},{4,8},{8,12},{12,16},{16,20},{20,24},{24,28},{28,32},{32,36}... | collective-permute-start | bytes 393224 | tf_op jit(solution)/shard_map/ppermute | solution.py:10
  39.0 64.3 %collective-permute-start.7 = (bf16[512,128]{1,0:T(8,128)(2,1)}, bf16[512,128]{1,0:T(8,128)(2,1)S(1)}, u32[]{:S(2)}, u32[]{:S(2)}) collective-permute-start(bf16[512,128]{1,0:T(8,128)(2,1)} %param.7), channel_id=1, source_target_pairs={{0,8},{4,12},{8,16},{12,20},{16,24},{20,28},{24,32},{28,36},{32,40... | collective-permute-start | bytes 393224 | tf_op jit(solution)/shard_map/ppermute | solution.py:10
  42.5 61.4 %collective-permute-start.8 = (bf16[512,128]{1,0:T(8,128)(2,1)}, bf16[512,128]{1,0:T(8,128)(2,1)S(1)}, u32[]{:S(2)}, u32[]{:S(2)}) collective-permute-start(bf16[512,128]{1,0:T(8,128)(2,1)} %param.7), channel_id=1, source_target_pairs={{0,16},{4,20},{8,24},{12,28},{16,32},{20,36},{24,40},{28,44},{32,4... | collective-permute-start | bytes 393224 | tf_op jit(solution)/shard_map/ppermute | solution.py:10
  47.6 57.0 %collective-permute-start.9 = (bf16[512,128]{1,0:T(8,128)(2,1)}, bf16[512,128]{1,0:T(8,128)(2,1)}, u32[]{:S(2)}, u32[]{:S(2)}) collective-permute-start(bf16[512,128]{1,0:T(8,128)(2,1)} %param.7), channel_id=1, source_target_pairs={{0,32},{4,36},{8,40},{12,44},{16,48},{20,52},{24,56},{28,60},{32,6... | collective-permute-start | bytes 393224 | tf_op jit(solution)/shard_map/ppermute | solution.py:10
  51.2 55.0 %collective-permute-start.10 = (bf16[512,128]{1,0:T(8,128)(2,1)}, bf16[512,128]{1,0:T(8,128)(2,1)}, u32[]{:S(2)}, u32[]{:S(2)}) collective-permute-start(bf16[512,128]{1,0:T(8,128)(2,1)} %param.7), channel_id=1, source_target_pairs={{0,64},{4,68},{8,72},{12,76},{16,80},{20,84},{24,88},{28,92},{32,9... | collective-permute-start | bytes 393224 | tf_op jit(solution)/shard_map/ppermute | solution.py:10
  54.3 6.2 %copy-start.2 = (bf16[3584,128]{1,0:T(8,128)(2,1)S(1)}, bf16[3584,128]{1,0:T(8,128)(2,1)}, u32[]{:S(2)}) copy-start(bf16[3584,128]{1,0:T(8,128)(2,1)} %constant_dynamic-update-slice_fusion) | copy-start | bytes 2752516
  82.7 18.6 %copy-start = (bf16[512,128]{1,0:T(8,128)(2,1)S(1)}, bf16[512,128]{1,0:T(8,128)(2,1)}, u32[]{:S(2)}) copy-start(bf16[512,128]{1,0:T(8,128)(2,1)} %param.7) | copy-start | bytes 393220
  82.7 25.7 %copy-start.4 = (f32[512]{0:T(512)S(1)}, f32[512]{0:T(512)}, u32[]{:S(2)}) copy-start(f32[512]{0:T(512)} %get-tuple-element.19) | copy-start | bytes 6148
  101.3 6.5 %collective-permute-start.11 = (bf16[512,128]{1,0:T(8,128)(2,1)S(1)}, bf16[512,128]{1,0:T(8,128)(2,1)S(1)}, u32[]{:S(2)}, u32[]{:S(2)}) collective-permute-start(bf16[512,128]{1,0:T(8,128)(2,1)S(1)} %copy-done), channel_id=1, source_target_pairs={{0,128},{4,132},{8,136},{12,140},{16,144},{20,148},{24,152},{28,15... | collective-permute-start | bytes 393224 | tf_op jit(solution)/shard_map/ppermute | solution.py:10
  107.7 6.7 %slice-start.6 = ((s8[7340032]{0:T(1024)(128)(4,1)}), s8[4194304]{0:T(1024)(128)(4,1)S(1)}, s32[]{:S(2)}) async-start(s8[7340032]{0:T(1024)(128)(4,1)} %bitcast.87), calls=%async_computation.7 | async-start | bytes 8388608
  107.7 6.7 %copy-start.6 = (f32[512]{0:T(512)S(1)}, f32[512]{0:T(512)}, u32[]{:S(2)}) copy-start(f32[512]{0:T(512)} %get-tuple-element.31) | copy-start | bytes 6148
  108.4 6.0 %copy-start.1 = (bf16[3584,128]{1,0:T(8,128)(2,1)S(1)}, bf16[3584,128]{1,0:T(8,128)(2,1)}, u32[]{:S(2)}) copy-start(bf16[3584,128]{1,0:T(8,128)(2,1)} %constant_dynamic-update-slice_fusion.7) | copy-start | bytes 2752516
  108.4 6.0 %slice-start.7 = ((s8[7340032]{0:T(1024)(128)(4,1)}), s8[3145728]{0:T(1024)(128)(4,1)S(1)}, s32[]{:S(2)}) async-start(s8[7340032]{0:T(1024)(128)(4,1)} %bitcast.87), calls=%async_computation.8 | async-start | bytes 6291456
  114.4 2.4 %slice-start.4 = ((s8[7340032]{0:T(1024)(128)(4,1)}), s8[4194304]{0:T(1024)(128)(4,1)S(1)}, s32[]{:S(2)}) async-start(s8[7340032]{0:T(1024)(128)(4,1)} %bitcast.85), calls=%async_computation.5 | async-start | bytes 8388608
  114.4 2.4 %copy-start.5 = (f32[512]{0:T(512)S(1)}, f32[512]{0:T(512)}, u32[]{:S(2)}) copy-start(f32[512]{0:T(512)} %get-tuple-element.29) | copy-start | bytes 6148
  114.5 3.1 %slice-start.5 = ((s8[7340032]{0:T(1024)(128)(4,1)}), s8[3145728]{0:T(1024)(128)(4,1)S(1)}, s32[]{:S(2)}) async-start(s8[7340032]{0:T(1024)(128)(4,1)} %bitcast.85), calls=%async_computation.6 | async-start | bytes 6291456
  116.8 3.1 %slice-start.2 = ((s8[7340032]{0:T(1024)(128)(4,1)}), s8[4194304]{0:T(1024)(128)(4,1)S(1)}, s32[]{:S(2)}) async-start(s8[7340032]{0:T(1024)(128)(4,1)} %bitcast.83), calls=%async_computation.3 | async-start | bytes 8388608
  116.8 3.1 %copy-start.3 = (f32[512]{0:T(512)S(1)}, f32[512]{0:T(512)}, u32[]{:S(2)}) copy-start(f32[512]{0:T(512)} %get-tuple-element.27) | copy-start | bytes 6148
  117.6 2.4 %slice-start.3 = ((s8[7340032]{0:T(1024)(128)(4,1)}), s8[3145728]{0:T(1024)(128)(4,1)S(1)}, s32[]{:S(2)}) async-start(s8[7340032]{0:T(1024)(128)(4,1)} %bitcast.83), calls=%async_computation.4 | async-start | bytes 6291456
  119.9 2.4 %slice-start = ((s8[7340032]{0:T(1024)(128)(4,1)}), s8[4194304]{0:T(1024)(128)(4,1)S(1)}, s32[]{:S(2)}) async-start(s8[7340032]{0:T(1024)(128)(4,1)} %bitcast.81), calls=%async_computation.1 | async-start | bytes 8388608
  120.0 3.0 %slice-start.1 = ((s8[7340032]{0:T(1024)(128)(4,1)}), s8[3145728]{0:T(1024)(128)(4,1)S(1)}, s32[]{:S(2)}) async-start(s8[7340032]{0:T(1024)(128)(4,1)} %bitcast.81), calls=%async_computation.2 | async-start | bytes 6291456
  127.6 2.5 %slice-start.8 = ((s8[6422528]{0:T(1024)(128)(4,1)}), s8[4194304]{0:T(1024)(128)(4,1)S(1)}, s32[]{:S(2)}) async-start(s8[6422528]{0:T(1024)(128)(4,1)} %bitcast.97), calls=%async_computation.9 | async-start | bytes 8388608
  127.6 2.9 %slice-start.9 = ((s8[6422528]{0:T(1024)(128)(4,1)}), s8[2228224]{0:T(1024)(128)(4,1)S(1)}, s32[]{:S(2)}) async-start(s8[6422528]{0:T(1024)(128)(4,1)} %bitcast.97), calls=%async_computation.10 | async-start | bytes 4456448
where the time goes:
time: 188 us; the launch traced here: 185 us
  matrix products  52.5 us (28%)
  blocking collectives  46.8 us (25%)
  starting transfers between devices  39.6 us (21%)
  other arithmetic  26.8 us (14%)
  local copies, waits for them, and re-layouts  19.1 us (10%)
    all_to_all x1, blocking collectives, sum_at_owner(): tiles = lax.all_to_all(split_up(x, dim, length), axis, 0, 0, tiled=True)  46.8 us
    ppermute x12, starting transfers between devices, passed_along(): return lax.ppermute(block, axis, route)  39.6 us
    dot_general x7, matrix products, per_device(): lax.dot_general(query_heads[:, head_id, :], keys_cat, (((1,), (1,)), ((),...  28.4 us
    dot_general x7, matrix products, per_device(): jnp.dot(weights, values_cat, preferred_element_type=jnp.float32)  19.9 us
    reduce_sum x1, other arithmetic, per_device(): row_total = jnp.sum(numerators, axis=-1)  18.5 us
    unnamed x52, local copies, waits for them, and re-layouts  15.9 us
    dot_general x1, matrix products, per_device(): jnp.dot(attended, out_weight, preferred_element_type=jnp.float32)  4.19 us
    and x6, other arithmetic, per_device(): usable = (block_id - offset >= 0) & (position < block_valid[source])  3.84 us
  transfers between devices with their start and end apart: 12, of which 0 were waited for; matrix products, arithmetic and copies ran while one was open for 37% of the time, Pallas kernels for 0%

commit v1 on v0

v1 whole, which is shorter than its diff:
```python
import contextlib
import math

import jax
import jax.numpy as jnp
from jax import lax
from jax.experimental import pallas as pl
from jax.experimental.pallas import tpu as pltpu
from jax.sharding import PartitionSpec as P

MESH = pl.DeviceIdType.MESH
TRACE = False
OWN, S1, S2, S4, S8, S16, S32, RELAY = range(8)
OFFSETS = {S1: 1, S2: 2, S4: 4, S8: 8, S16: 16, S32: 32}


def scope(name):
    return jax.named_scope(name) if TRACE else contextlib.nullcontext()


def kernel(
    valid_ref, q_hbm, k_hbm, v_hbm, w_hbm, o_hbm,
    q_s, kv, vt, w_s, acc, m_s, att, own_s, out_s,
    far_send, far_recv, near_send, near_recv,
    load_sem, w_sem, kv_send, kv_recv, fs_sem, fr_sem, ns_sem, nr_sem, out_sem,
):
    rows, qcols = q_hbm.shape
    hd = k_hbm.shape[1]
    heads = qcols // hd
    chunk = rows // 4
    pw = out_s.shape[2]
    np_ = out_s.shape[0]
    half = np_ // 2
    c = lax.axis_index("ctx")
    h = lax.axis_index("kvh")
    core = lax.rem(c, 2)
    y = lax.rem(c // 2, 4)
    z = c // 8

    def at(dz, dy):
        return lax.rem(z + 8 + dz, 8) * 8 + lax.rem(y + 4 + dy, 4) * 2 + core

    right, left = lax.rem(h + 1, 4), lax.rem(h + 3, 4)
    partner = c + 1 - 2 * core

    chunk_ids = [lax.rem(h + 2, 4), right, left, h]
    loads = []
    k_load = pltpu.make_async_copy(k_hbm, kv.at[OWN, 0], load_sem.at[0])
    v_load = pltpu.make_async_copy(v_hbm, kv.at[OWN, 1], load_sem.at[1])
    k_load.start()
    v_load.start()
    for i, cid in enumerate(chunk_ids):
        src = q_hbm.at[pl.ds(pl.multiple_of(cid * chunk, chunk), chunk), :]
        cp = pltpu.make_async_copy(src, q_s.at[pl.ds(i * chunk, chunk), :], load_sem.at[2 + i])
        cp.start()
        loads.append(cp)
    w_load = pltpu.make_async_copy(w_hbm, w_s, w_sem)
    w_load.start()

    barrier = pltpu.get_barrier_semaphore()
    senders = [
        (at(-1, 0), h), (at(1, 0), h), (at(-2, 0), h), (at(3, 0), h),
        (at(0, -1), h), (at(0, -2), h), (partner, h), (c, left), (c, right),
    ]
    with scope("entry"):
        for dev in senders:
            pl.semaphore_signal(barrier, inc=1, device_id=dev, device_id_type=MESH)
        pl.semaphore_wait(barrier, len(senders))

    def kv_copy(src_slot, dst_slot, part, dev):
        return pltpu.make_async_remote_copy(
            src_ref=kv.at[src_slot, part], dst_ref=kv.at[dst_slot, part],
            send_sem=kv_send.at[dst_slot, part], recv_sem=kv_recv.at[dst_slot, part],
            device_id=dev, device_id_type=MESH,
        )

    def arrived(slot, part):
        with scope(f"wait_{slot}_{part}"):
            kv_copy(OWN, slot, part, (c, h)).wait_recv()

    z_up, z_up2, z_down, z_down3 = (at(1, 0), h), (at(2, 0), h), (at(-1, 0), h), (at(-3, 0), h)
    y_up, y_up2 = (at(0, 1), h), (at(0, 2), h)
    other = (partner, h)

    k_load.wait()
    v_load.wait()
    kv_copy(OWN, S8, 0, z_up).start()
    kv_copy(OWN, RELAY, 1, z_down).start()
    kv_copy(OWN, S8, 1, z_up).start()

    @pl.when(y < 3)
    def _():
        kv_copy(OWN, S2, 0, y_up).start()
        kv_copy(OWN, S2, 1, y_up).start()

    @pl.when(y < 2)
    def _():
        kv_copy(OWN, S4, 0, y_up2).start()
        kv_copy(OWN, S4, 1, y_up2).start()

    @pl.when(core == 0)
    def _():
        kv_copy(OWN, S1, 0, other).start()
        kv_copy(OWN, S1, 1, other).start()

    scale = hd ** -0.5 * math.log2(math.e)
    blk_valid = valid_ref[c]
    ones_rows = vt.shape[0] - hd
    vt[pl.ds(hd, ones_rows), :] = jnp.ones((ones_rows, rows), vt.dtype)
    acc[...] = jnp.zeros_like(acc)
    m_s[...] = jnp.full_like(m_s, -1e30)

    def block_step(slot, pair, g, diag):
        q = q_s[pl.ds(pl.multiple_of(pair * 2 * chunk, 2 * chunk), 2 * chunk), g * hd:(g + 1) * hd]
        s = lax.dot_general(
            kv[slot, 0], q, (((1,), (1,)), ((), ())), preferred_element_type=jnp.float32
        )
        if diag:
            key_at = lax.broadcasted_iota(jnp.int32, s.shape, 0)
            col = lax.broadcasted_iota(jnp.int32, s.shape, 1)
            first = jnp.where(pair == 0, chunk_ids[0], chunk_ids[2])
            second = jnp.where(pair == 0, chunk_ids[1], chunk_ids[3])
            query_at = jnp.where(col < chunk, first * chunk + col, second * chunk + col - chunk)
            s = jnp.where((key_at <= query_at) & (key_at < blk_valid), s, -1e30)
        m_old = m_s[pair, g, 0:1, :]
        m_new = jnp.maximum(m_old, jnp.max(s, axis=0, keepdims=True))
        p = jnp.exp2((s - m_new) * scale).astype(jnp.bfloat16)
        alpha = jnp.exp2((m_old - m_new) * scale)
        pv = jnp.dot(vt[...], p, preferred_element_type=jnp.float32)
        acc[pair, g] = acc[pair, g] * alpha + pv
        m_s[pair, g] = jnp.broadcast_to(m_new, m_s.shape[2:])

    def set_vt(slot):
        vt[pl.ds(0, hd), :] = kv[slot, 1].T

    def block(slot, pair, diag=False):
        for g in range(heads):
            block_step(slot, pair, g, diag)

    def both(slot, diag=False):
        with scope(f"both_{slot}"):
            set_vt(slot)

            @pl.loop(0, 2)
            def _(pair):
                block(slot, pair, diag)

    with scope("blk_own"):
        for cp in loads:
            cp.wait()
        both(OWN, diag=True)

    for part in range(2):
        arrived(S8, part)
        kv_copy(S8, S16, part, z_up).start()

        @pl.when(y == 3)
        def _():
            kv_copy(S8, S2, part, y_up).start()

        @pl.when(y >= 2)
        def _():
            kv_copy(S8, S4, part, y_up2).start()

    arrived(RELAY, 1)
    kv_copy(RELAY, S32, 1, z_down3).start()

    @pl.when(c >= 8)
    def _():
        both(S8)

    for part in range(2):
        arrived(S2, part)

        @pl.when(core == 1)
        def _():
            kv_copy(S2, S1, part, other).start()

    @pl.when(c >= 2)
    def _():
        both(S2)

    arrived(S16, 0)
    kv_copy(S16, S32, 0, z_up2).start()

    for slot in (S1, S4, S16):
        arrived(slot, 1)
        if slot != S16:
            arrived(slot, 0)

        @pl.when(c >= OFFSETS[slot])
        def _():
            both(slot)

    arrived(S32, 0)
    arrived(S32, 1)

    @pl.when(c >= 32)
    def _():
        with scope("last_0"):
            set_vt(S32)
            block(S32, 0)

    def finish(pair):
        for g in range(heads):
            full = acc[pair, g]
            mix = full[:hd, :] / full[hd:hd + 1, :]
            att[pl.ds(pl.multiple_of(pair * 2 * chunk, 2 * chunk), 2 * chunk), g * hd:(g + 1) * hd] = (
                mix.T.astype(jnp.bfloat16)
            )

    def partial(i, piece):
        cols = pl.ds(pl.multiple_of(piece * pw, pw), pw)
        return jnp.dot(
            att[i * chunk:(i + 1) * chunk, :], w_s[:, cols], preferred_element_type=jnp.float32
        )

    def far_copy(side, j):
        piece = j if side == 0 else half + j
        return pltpu.make_async_remote_copy(
            src_ref=far_send.at[piece], dst_ref=far_recv.at[side, j],
            send_sem=fs_sem.at[side, j], recv_sem=fr_sem.at[side, j],
            device_id=(c, right if side == 0 else left), device_id_type=MESH,
        )

    def near_copy(side, piece):
        return pltpu.make_async_remote_copy(
            src_ref=near_send.at[side, piece], dst_ref=near_recv.at[side, piece],
            send_sem=ns_sem.at[side, piece], recv_sem=nr_sem.at[side, piece],
            device_id=(c, right if side == 0 else left), device_id_type=MESH,
        )

    with scope("finish_0"):
        finish(0)
        w_load.wait()

    with scope("far"):
        @pl.loop(0, half)
        def _(j):
            far_send[j] = partial(0, j).astype(jnp.bfloat16)
            far_copy(0, j).start()
            far_send[half + j] = partial(0, half + j).astype(jnp.bfloat16)
            far_copy(1, j).start()

    @pl.when(c >= 32)
    def _():
        with scope("last_1"):
            block(S32, 1)

    with scope("finish_1"):
        finish(1)

    with scope("near_plain"):
        @pl.loop(0, half)
        def _(j):
            near_send[0, half + j] = partial(1, half + j).astype(jnp.bfloat16)
            near_copy(0, half + j).start()
            near_send[1, j] = partial(2, j).astype(jnp.bfloat16)
            near_copy(1, j).start()

    with scope("own_part"):
        @pl.loop(0, np_)
        def _(j):
            own_s[j] = partial(3, j)

    with scope("near_sum"):
        @pl.loop(0, half)
        def _(j):
            mine = partial(1, j)
            far_copy(0, j).wait_recv()
            near_send[0, j] = (mine + far_recv[0, j].astype(jnp.float32)).astype(jnp.bfloat16)
            near_copy(0, j).start()
            mine = partial(2, half + j)
            far_copy(1, j).wait_recv()
            near_send[1, half + j] = (mine + far_recv[1, j].astype(jnp.float32)).astype(jnp.bfloat16)
            near_copy(1, half + j).start()

    def out_copy(piece):
        return pltpu.make_async_copy(
            out_s.at[piece], o_hbm.at[:, pl.ds(pl.multiple_of(piece * pw, pw), pw)], out_sem.at[piece]
        )

    def final(piece):
        near_copy(0, piece).wait_recv()
        near_copy(1, piece).wait_recv()
        out_s[piece] = (
            own_s[piece] + near_recv[0, piece].astype(jnp.float32) + near_recv[1, piece].astype(jnp.float32)
        ).astype(out_s.dtype)
        out_copy(piece).start()

    with scope("final"):
        @pl.loop(0, half)
        def _(j):
            final(j)
            final(half + j)

    for slot in (S2, S4, S1, S8, S16, S32):
        for part in range(2):
            kv_copy(OWN, slot, part, (c, h)).wait_send()
    kv_copy(OWN, RELAY, 1, (c, h)).wait_send()

    @pl.loop(0, half)
    def _(j):
        far_copy(0, j).wait_send()
        far_copy(1, j).wait_send()

    @pl.loop(0, np_)
    def _(j):
        near_copy(0, j).wait_send()
        near_copy(1, j).wait_send()
        out_copy(j).wait()


def per_device(queries, key_block, value_block, block_valid, out_weight):
    rows, qcols = queries.shape
    hd = key_block.shape[1]
    heads = qcols // hd
    d = out_weight.shape[1]
    chunk = rows // 4
    pw = 256
    np_ = d // pw
    half = np_ // 2
    bf16, f32 = jnp.bfloat16, jnp.float32
    any_spec = pl.BlockSpec(memory_space=pl.ANY)
    return pl.pallas_call(
        kernel,
        out_shape=jax.ShapeDtypeStruct((chunk, d), bf16),
        in_specs=[pl.BlockSpec(memory_space=pltpu.SMEM)] + [any_spec] * 4,
        out_specs=any_spec,
        scratch_shapes=[
            pltpu.VMEM((rows, qcols), bf16),
            pltpu.VMEM((8, 2, rows, hd), bf16),
            pltpu.VMEM((hd + 16, rows), bf16),
            pltpu.VMEM((qcols, d), bf16),
            pltpu.VMEM((2, heads, hd + 16, 2 * chunk), f32),
            pltpu.VMEM((2, heads, 8, 2 * chunk), f32),
            pltpu.VMEM((rows, qcols), bf16),
            pltpu.VMEM((np_, chunk, pw), f32),
            pltpu.VMEM((np_, chunk, pw), bf16),
            pltpu.VMEM((np_, chunk, pw), bf16),
            pltpu.VMEM((2, half, chunk, pw), bf16),
            pltpu.VMEM((2, np_, chunk, pw), bf16),
            pltpu.VMEM((2, np_, chunk, pw), bf16),
            pltpu.SemaphoreType.DMA((6,)),
            pltpu.SemaphoreType.DMA,
            pltpu.SemaphoreType.DMA((8, 2)),
            pltpu.SemaphoreType.DMA((8, 2)),
            pltpu.SemaphoreType.DMA((2, half)),
            pltpu.SemaphoreType.DMA((2, half)),
            pltpu.SemaphoreType.DMA((2, np_)),
            pltpu.SemaphoreType.DMA((2, np_)),
            pltpu.SemaphoreType.DMA((np_,)),
        ],
        compiler_params=pltpu.CompilerParams(
            collective_id=0, has_side_effects=True, vmem_limit_bytes=67_043_328
        ),
        name="attend_project",
    )(block_valid, queries, key_block, value_block, out_weight)


def solution(mesh):
    return jax.shard_map(
        per_device,
        mesh=mesh,
        in_specs=(P("ctx", "kvh"), P("ctx", "kvh"), P("ctx", "kvh"), P(), P("kvh", None)),
        out_specs=P(("ctx", "kvh"), None),
        check_vma=False,
    )
```

time: 188 us -> 89.6 us (0.48)
  the two profiles are of different devices: /device:TPU:8 before, /device:TPU:160 now
where the time goes in v1:
time: 89.6 us; the launch traced here: 89.5 us
  Pallas kernels  87.3 us (97%)
  local copies, waits for them, and re-layouts  2.16 us (2%)
    pallas_call x1, Pallas kernels, per_device(): pl.pallas_call(kernel, out_shape=jax.ShapeDtypeStruct((chunk, d), bf16),...  87.3 us
    unnamed x1, local copies, waits for them, and re-layouts  2.16 us

profile of v1, /device:TPU:160, one launch (start us, length us, event | category | flops | bytes accessed | tf_op | source)
XLA Modules:
  0.0 89.5 jit_solution(6206723825872822029)
XLA Ops:
  0.0 87.3 %attend_project.1 = bf16[128,3584]{1,0:T(8,128)(2,1)} custom-call(s32[64]{0:T(128)} %valid_ref.1, bf16[512,896]{1,0:T(8,128)(2,1)} %q_hbm.1, bf16[512,128]{1,0:T(8,128)(2,1)} %k_hbm.1, bf16[512,128]{1,0:T(8,128)(2,1)} %v_hbm.1, bf16[896,3584]{1,0:T(8,128)(2,1)} %w_hbm.1), custom_call_target="tpu_custom_call" | custom-call | tf_op jit(solution)/shard_map/attend_project/pallas_call | solution.py:325
  87.3 2.2 %copy.7 = bf16[128,3584]{1,0:T(8,128)(2,1)} copy(bf16[128,3584]{1,0:T(8,128)(2,1)} %attend_project.1) | data formatting | bytes 1835008

commit v2 on v1

v2 whole, which is shorter than its diff:
```python
import contextlib
import math

import jax
import jax.numpy as jnp
from jax import lax
from jax.experimental import pallas as pl
from jax.experimental.pallas import tpu as pltpu
from jax.sharding import PartitionSpec as P

MESH = pl.DeviceIdType.MESH
TRACE = False
OWN, S1, S2, S4, S8, S16, S32, RELAY, RELAY_Y = range(9)
OFFSETS = {S1: 1, S2: 2, S4: 4, S8: 8, S16: 16, S32: 32}


def scope(name):
    return jax.named_scope(name) if TRACE else contextlib.nullcontext()


def kernel(
    valid_ref, q_hbm, k_hbm, v_hbm, w_hbm, o_hbm,
    q_s, kv, vt, w_s, acc, m_s, s_s, p_s, alpha_s, att, own_s, out_s,
    far_send, far_recv, near_send, near_recv,
    load_sem, w_sem, kv_send, kv_recv, fs_sem, fr_sem, ns_sem, nr_sem, out_sem,
):
    rows, qcols = q_hbm.shape
    hd = k_hbm.shape[1]
    heads = qcols // hd
    chunk = rows // 4
    pw = out_s.shape[2]
    np_ = out_s.shape[0]
    half = np_ // 2
    c = lax.axis_index("ctx")
    h = lax.axis_index("kvh")
    core = lax.rem(c, 2)
    y = lax.rem(c // 2, 4)
    z = c // 8

    def at(dz, dy):
        return lax.rem(z + 8 + dz, 8) * 8 + lax.rem(y + 4 + dy, 4) * 2 + core

    right, left = lax.rem(h + 1, 4), lax.rem(h + 3, 4)
    partner = c + 1 - 2 * core

    chunk_ids = [lax.rem(h + 2, 4), right, left, h]
    loads = []
    k_load = pltpu.make_async_copy(k_hbm, kv.at[OWN, 0], load_sem.at[0])
    v_load = pltpu.make_async_copy(v_hbm, kv.at[OWN, 1], load_sem.at[1])
    k_load.start()
    v_load.start()
    for i, cid in enumerate(chunk_ids):
        src = q_hbm.at[pl.ds(pl.multiple_of(cid * chunk, chunk), chunk), :]
        cp = pltpu.make_async_copy(src, q_s.at[pl.ds(i * chunk, chunk), :], load_sem.at[2 + i])
        cp.start()
        loads.append(cp)
    w_load = pltpu.make_async_copy(w_hbm, w_s, w_sem)
    w_load.start()

    barrier = pltpu.get_barrier_semaphore()
    senders = [
        (at(-1, 0), h), (at(1, 0), h), (at(-2, 0), h), (at(3, 0), h),
        (at(0, -1), h), (at(0, 1), h), (partner, h), (c, left), (c, right),
    ]
    with scope("entry"):
        for dev in senders:
            pl.semaphore_signal(barrier, inc=1, device_id=dev, device_id_type=MESH)
        pl.semaphore_wait(barrier, len(senders))

    def kv_copy(src_slot, dst_slot, part, dev, sent_as=None):
        return pltpu.make_async_remote_copy(
            src_ref=kv.at[src_slot, part], dst_ref=kv.at[dst_slot, part],
            send_sem=kv_send.at[dst_slot if sent_as is None else sent_as, part],
            recv_sem=kv_recv.at[dst_slot, part],
            device_id=dev, device_id_type=MESH,
        )

    def arrived(slot, part):
        with scope(f"wait_{slot}_{part}"):
            kv_copy(OWN, slot, part, (c, h)).wait_recv()

    z_up, z_up2, z_down, z_down3 = (at(1, 0), h), (at(2, 0), h), (at(-1, 0), h), (at(-3, 0), h)
    y_up, y_down = (at(0, 1), h), (at(0, -1), h)
    other = (partner, h)

    k_load.wait()
    v_load.wait()
    kv_copy(OWN, S8, 0, z_up).start()
    kv_copy(OWN, RELAY, 1, z_down).start()
    kv_copy(OWN, S8, 1, z_up).start()

    @pl.when(y < 3)
    def _():
        kv_copy(OWN, S2, 0, y_up).start()
        kv_copy(OWN, S2, 1, y_up).start()

    @pl.when(core == 0)
    def _():
        kv_copy(OWN, S1, 0, other).start()
        kv_copy(OWN, S1, 1, other).start()

    scale = hd ** -0.5 * math.log2(math.e)
    blk_valid = valid_ref[c]
    ones_rows = vt.shape[1] - hd
    vt[:, hd:, :] = jnp.ones((vt.shape[0], ones_rows, rows), vt.dtype)
    acc[...] = jnp.zeros_like(acc)
    m_s[...] = jnp.full_like(m_s, -1e30)

    sub = rows // 2

    def tile_scores(slot, t, diag):
        pair, g = divmod(t, heads)
        q = q_s[pair * 2 * chunk:(pair + 1) * 2 * chunk, g * hd:(g + 1) * hd]
        m_old = m_s[t, 0:1, :]
        m_new = m_old
        for i in range(0, rows, sub):
            s = lax.dot_general(
                kv[slot, 0, i:i + sub, :], q, (((1,), (1,)), ((), ())), preferred_element_type=jnp.float32
            )
            if diag:
                key_at = i + lax.broadcasted_iota(jnp.int32, s.shape, 0)
                col = lax.broadcasted_iota(jnp.int32, s.shape, 1)
                first, second = chunk_ids[2 * pair], chunk_ids[2 * pair + 1]
                query_at = jnp.where(col < chunk, first * chunk + col, second * chunk + col - chunk)
                s = jnp.where((key_at <= query_at) & (key_at < blk_valid), s, -1e30)
            s_s[t % 2, i:i + sub] = s
            m_new = jnp.maximum(m_new, jnp.max(s, axis=0, keepdims=True))
        alpha_s[t % 3] = jnp.broadcast_to(jnp.exp2((m_old - m_new) * scale), alpha_s.shape[1:])
        m_s[t] = jnp.broadcast_to(m_new, m_s.shape[1:])

    def tile_weights(t):
        m = m_s[t, 0:1, :]
        for i in range(0, rows, sub):
            p_s[t % 2, i:i + sub] = jnp.exp2((s_s[t % 2, i:i + sub] - m) * scale).astype(p_s.dtype)

    def tile_mix(slot, t):
        pv = jnp.dot(vt[slot], p_s[t % 2], preferred_element_type=jnp.float32)
        acc[t] = acc[t] * alpha_s[t % 3, 0:1, :] + pv

    def tiles(slot, lo, hi, diag=False):
        tile_scores(slot, lo, diag)
        for t in range(lo, hi + 1):
            if t + 1 < hi:
                tile_scores(slot, t + 1, diag)
            if t < hi:
                tile_weights(t)
            if t > lo:
                tile_mix(slot, t - 1)

    def set_vt(slot):
        vt[slot, 0:hd, :] = kv[slot, 1].T

    def first_pair(slot):
        @pl.when(c >= OFFSETS[slot])
        def _():
            with scope(f"p0_{slot}"):
                set_vt(slot)
                tiles(slot, 0, heads)

    def second_pair(slot):
        @pl.when(c >= OFFSETS[slot])
        def _():
            with scope(f"p1_{slot}"):
                tiles(slot, heads, 2 * heads)

    with scope("blk_own"):
        for cp in loads:
            cp.wait()
        set_vt(OWN)
        tiles(OWN, 0, 2 * heads, True)

    for part in range(2):
        arrived(S8, part)
        kv_copy(S8, S16, part, z_up).start()

        @pl.when(y == 3)
        def _():
            kv_copy(S8, S2, part, y_up).start()

        @pl.when(y == 2)
        def _():
            kv_copy(S8, RELAY_Y, part, y_down).start()

    arrived(RELAY, 1)
    kv_copy(RELAY, S32, 1, z_down3).start()

    def pass_on_s2():
        for part in range(2):
            arrived(S2, part)

            @pl.when(core == 1)
            def _():
                kv_copy(S2, S1, part, other).start()

            @pl.when(y < 3)
            def _():
                kv_copy(S2, S4, part, y_up).start()

    pl.when(y > 0)(pass_on_s2)

    @pl.when(c >= OFFSETS[S8])
    def _():
        with scope("both_s8"):
            set_vt(S8)
            tiles(S8, 0, 2 * heads)

    arrived(S16, 0)
    kv_copy(S16, S32, 0, z_up2).start()
    pl.when(y == 0)(pass_on_s2)

    @pl.when(y == 1)
    def _():
        for part in range(2):
            arrived(RELAY_Y, part)
            kv_copy(RELAY_Y, S4, part, y_down, sent_as=RELAY_Y).start()

    first_pair(S2)
    for slot in (S1, S16):
        arrived(slot, 1)
        if slot != S16:
            arrived(slot, 0)
        first_pair(slot)

    @pl.when(y > 0)
    def _():
        second_pair(S2)

    for slot in (S4, S32):
        arrived(slot, 0)
        arrived(slot, 1)
        first_pair(slot)

    def finish(pair):
        for g in range(heads):
            full = acc[pair * heads + g]
            mix = full[:hd, :] / full[hd:hd + 1, :]
            att[pair * 2 * chunk:(pair + 1) * 2 * chunk, g * hd:(g + 1) * hd] = mix.T.astype(jnp.bfloat16)

    def partial(i, piece):
        cols = pl.ds(piece * pw if isinstance(piece, int) else pl.multiple_of(piece * pw, pw), pw)
        return jnp.dot(
            att[i * chunk:(i + 1) * chunk, :], w_s[:, cols], preferred_element_type=jnp.float32
        )

    def far_copy(side, j):
        piece = j if side == 0 else half + j
        return pltpu.make_async_remote_copy(
            src_ref=far_send.at[piece], dst_ref=far_recv.at[side, j],
            send_sem=fs_sem.at[side, j], recv_sem=fr_sem.at[side, j],
            device_id=(c, right if side == 0 else left), device_id_type=MESH,
        )

    def near_copy(side, piece):
        return pltpu.make_async_remote_copy(
            src_ref=near_send.at[side, piece], dst_ref=near_recv.at[side, piece],
            send_sem=ns_sem.at[side, piece], recv_sem=nr_sem.at[side, piece],
            device_id=(c, right if side == 0 else left), device_id_type=MESH,
        )

    with scope("finish_0"):
        finish(0)
        w_load.wait()

    bf16 = jnp.bfloat16

    with scope("far"):

        @pl.loop(0, half)
        def _(j):
            low, high = partial(0, j), partial(0, half + j)
            far_send[j] = low.astype(bf16)
            far_send[half + j] = high.astype(bf16)
            far_copy(0, j).start()
            far_copy(1, j).start()

    def plain(side, pieces):
        for at_piece in range(0, len(pieces), 2):
            group = pieces[at_piece:at_piece + 2]
            parts = [partial(1 + side, piece) for piece in group]
            for piece, value in zip(group, parts):
                near_send[side, piece] = value.astype(bf16)
            for piece in group:
                near_copy(side, piece).start()

    with scope("plain_right"):
        plain(0, list(range(half, np_)))

    @pl.when(y == 0)
    def _():
        second_pair(S2)

    for slot in (S1, S16, S4, S32):
        second_pair(slot)

    with scope("finish_1"):
        finish(1)

    with scope("plain_left"):
        plain(1, list(range(half)))

    with scope("near_sum"):

        @pl.loop(0, half)
        def _(j):
            low, high = partial(1, j), partial(2, half + j)
            far_copy(0, j).wait_recv()
            near_send[0, j] = (low + far_recv[0, j].astype(jnp.float32)).astype(bf16)
            near_copy(0, j).start()
            far_copy(1, j).wait_recv()
            near_send[1, half + j] = (high + far_recv[1, j].astype(jnp.float32)).astype(bf16)
            near_copy(1, half + j).start()

    with scope("own_part"):

        @pl.loop(0, half)
        def _(j):
            low, high = partial(3, j), partial(3, half + j)
            own_s[j] = low
            own_s[half + j] = high

    def out_copy(piece):
        return pltpu.make_async_copy(
            out_s.at[piece], o_hbm.at[:, pl.ds(pl.multiple_of(piece * pw, pw), pw)], out_sem.at[piece]
        )

    def final(piece):
        near_copy(0, piece).wait_recv()
        near_copy(1, piece).wait_recv()
        out_s[piece] = (
            own_s[piece] + near_recv[0, piece].astype(jnp.float32) + near_recv[1, piece].astype(jnp.float32)
        ).astype(out_s.dtype)
        out_copy(piece).start()

    with scope("final"):
        @pl.loop(0, half)
        def _(j):
            final(j)
            final(half + j)

    for part in range(2):
        for slot in (S2, S1, S8, S16, S32):
            kv_copy(OWN, slot, part, (c, h)).wait_send()

        @pl.when(y < 3)
        def _():
            kv_copy(OWN, S4, part, (c, h)).wait_send()

        @pl.when((y == 1) | (y == 2))
        def _():
            kv_copy(OWN, RELAY_Y, part, (c, h)).wait_send()
    kv_copy(OWN, RELAY, 1, (c, h)).wait_send()

    @pl.loop(0, half)
    def _(j):
        far_copy(0, j).wait_send()
        far_copy(1, j).wait_send()

    @pl.loop(0, np_)
    def _(j):
        near_copy(0, j).wait_send()
        near_copy(1, j).wait_send()
        out_copy(j).wait()


def per_device(queries, key_block, value_block, block_valid, out_weight):
    rows, qcols = queries.shape
    hd = key_block.shape[1]
    heads = qcols // hd
    d = out_weight.shape[1]
    chunk = rows // 4
    pw = 256
    np_ = d // pw
    half = np_ // 2
    bf16, f32 = jnp.bfloat16, jnp.float32
    any_spec = pl.BlockSpec(memory_space=pl.ANY)
    return pl.pallas_call(
        kernel,
        out_shape=jax.ShapeDtypeStruct((chunk, d), bf16),
        in_specs=[pl.BlockSpec(memory_space=pltpu.SMEM)] + [any_spec] * 4,
        out_specs=any_spec,
        scratch_shapes=[
            pltpu.VMEM((rows, qcols), bf16),
            pltpu.VMEM((9, 2, rows, hd), bf16),
            pltpu.VMEM((7, hd + 16, rows), bf16),
            pltpu.VMEM((qcols, d), bf16),
            pltpu.VMEM((2 * heads, hd + 16, 2 * chunk), f32),
            pltpu.VMEM((2 * heads, 8, 2 * chunk), f32),
            pltpu.VMEM((2, rows, 2 * chunk), f32),
            pltpu.VMEM((2, rows, 2 * chunk), bf16),
            pltpu.VMEM((3, 8, 2 * chunk), f32),
            pltpu.VMEM((rows, qcols), bf16),
            pltpu.VMEM((np_, chunk, pw), f32),
            pltpu.VMEM((np_, chunk, pw), bf16),
            pltpu.VMEM((np_, chunk, pw), bf16),
            pltpu.VMEM((2, half, chunk, pw), bf16),
            pltpu.VMEM((2, np_, chunk, pw), bf16),
            pltpu.VMEM((2, np_, chunk, pw), bf16),
            pltpu.SemaphoreType.DMA((6,)),
            pltpu.SemaphoreType.DMA,
            pltpu.SemaphoreType.DMA((9, 2)),
            pltpu.SemaphoreType.DMA((9, 2)),
            pltpu.SemaphoreType.DMA((2, half)),
            pltpu.SemaphoreType.DMA((2, half)),
            pltpu.SemaphoreType.DMA((2, np_)),
            pltpu.SemaphoreType.DMA((2, np_)),
            pltpu.SemaphoreType.DMA((np_,)),
        ],
        compiler_params=pltpu.CompilerParams(
            collective_id=0, has_side_effects=True, vmem_limit_bytes=67_043_328
        ),
        name="attend_project",
    )(block_valid, queries, key_block, value_block, out_weight)


def solution(mesh):
    return jax.shard_map(
        per_device,
        mesh=mesh,
        in_specs=(P("ctx", "kvh"), P("ctx", "kvh"), P("ctx", "kvh"), P(), P("kvh", None)),
        out_specs=P(("ctx", "kvh"), None),
        check_vma=False,
    )
```

time: 89.6 us -> 62.9 us (0.70)
  the two profiles are of different devices: /device:TPU:160 before, /device:TPU:8 now
where the time goes in v2:
time: 62.9 us; the launch traced here: 62.3 us
  Pallas kernels  60.1 us (96%)
  local copies, waits for them, and re-layouts  2.16 us (3%)
    pallas_call x1, Pallas kernels, per_device(): pl.pallas_call(kernel, out_shape=jax.ShapeDtypeStruct((chunk, d), bf16),...  60.1 us
    unnamed x1, local copies, waits for them, and re-layouts  2.16 us

profile of v2, /device:TPU:8, one launch (start us, length us, event | category | flops | bytes accessed | tf_op | source)
XLA Modules:
  0.0 62.3 jit_solution(5619844755225021307)
XLA Ops:
  0.0 60.1 %attend_project.1 = bf16[128,3584]{1,0:T(8,128)(2,1)} custom-call(s32[64]{0:T(128)} %valid_ref.1, bf16[512,896]{1,0:T(8,128)(2,1)} %q_hbm.1, bf16[512,128]{1,0:T(8,128)(2,1)} %k_hbm.1, bf16[512,128]{1,0:T(8,128)(2,1)} %v_hbm.1, bf16[896,3584]{1,0:T(8,128)(2,1)} %w_hbm.1), custom_call_target="tpu_custom_call" | custom-call | tf_op jit(solution)/shard_map/attend_project/pallas_call | solution.py:376
  60.1 2.2 %copy.7 = bf16[128,3584]{1,0:T(8,128)(2,1)} copy(bf16[128,3584]{1,0:T(8,128)(2,1)} %attend_project.1) | data formatting | bytes 1835008

commit v3 on v2

--- a/solution.py
+++ b/solution.py
@@ -19,17 +19,17 @@
 
 
 def kernel(
-    valid_ref, q_hbm, k_hbm, v_hbm, w_hbm, o_hbm,
-    q_s, kv, vt, w_s, acc, m_s, s_s, p_s, alpha_s, att, own_s, out_s,
+    valid_ref, q_hbm, k_hbm, v_hbm, w_hbm, o_ref,
+    q_s, kv, vt, w_s, acc, m_s, s_s, p_s, alpha_s, att, own_s,
     far_send, far_recv, near_send, near_recv,
-    load_sem, w_sem, kv_send, kv_recv, fs_sem, fr_sem, ns_sem, nr_sem, out_sem,
+    load_sem, w_sem, kv_send, kv_recv, cut_send, cut_recv, fs_sem, fr_sem, ns_sem, nr_sem,
 ):
     rows, qcols = q_hbm.shape
     hd = k_hbm.shape[1]
     heads = qcols // hd
     chunk = rows // 4
-    pw = out_s.shape[2]
-    np_ = out_s.shape[0]
+    pw = own_s.shape[2]
+    np_ = own_s.shape[0]
     half = np_ // 2
     c = lax.axis_index("ctx")
     h = lax.axis_index("kvh")
@@ -79,6 +79,17 @@
         with scope(f"wait_{slot}_{part}"):
             kv_copy(OWN, slot, part, (c, h)).wait_recv()
 
+    cut = rows * 3 // 4
+
+    def cut_copy(src_slot, dst_slot, dev, low):
+        part_rows = pl.ds(0, cut) if low else pl.ds(cut, rows - cut)
+        sem = 0 if low else 1 if dst_slot == RELAY else 2
+        return pltpu.make_async_remote_copy(
+            src_ref=kv.at[src_slot, 0, part_rows], dst_ref=kv.at[dst_slot, 0, part_rows],
+            send_sem=cut_send.at[sem], recv_sem=cut_recv.at[sem],
+            device_id=dev, device_id_type=MESH,
+        )
+
     z_up, z_up2, z_down, z_down3 = (at(1, 0), h), (at(2, 0), h), (at(-1, 0), h), (at(-3, 0), h)
     y_up, y_down = (at(0, 1), h), (at(0, -1), h)
     other = (partner, h)
@@ -87,6 +98,7 @@
     v_load.wait()
     kv_copy(OWN, S8, 0, z_up).start()
     kv_copy(OWN, RELAY, 1, z_down).start()
+    cut_copy(OWN, RELAY, z_down, False).start()
     kv_copy(OWN, S8, 1, z_up).start()
 
     @pl.when(y < 3)
@@ -169,7 +181,13 @@
         set_vt(OWN)
         tiles(OWN, 0, 2 * heads, True)
 
-    for part in range(2):
+    @pl.when(core == 1)
+    def _():
+        arrived(S1, 0)
+        arrived(S1, 1)
+        first_pair(S1)
+
+    def pass_on_s8(part):
         arrived(S8, part)
         kv_copy(S8, S16, part, z_up).start()
 
@@ -181,8 +199,17 @@
         def _():
             kv_copy(S8, RELAY_Y, part, y_down).start()
 
+    pass_on_s8(0)
     arrived(RELAY, 1)
     kv_copy(RELAY, S32, 1, z_down3).start()
+    cut_copy(OWN, RELAY, (c, h), False).wait_recv()
+    cut_copy(RELAY, S32, z_down3, False).start()
+
+    @pl.when(core == 1)
+    def _():
+        second_pair(S1)
+
+    pass_on_s8(1)
 
     def pass_on_s2():
         for part in range(2):
@@ -205,7 +232,7 @@
             tiles(S8, 0, 2 * heads)
 
     arrived(S16, 0)
-    kv_copy(S16, S32, 0, z_up2).start()
+    cut_copy(S16, S32, z_up2, True).start()
     pl.when(y == 0)(pass_on_s2)
 
     @pl.when(y == 1)
@@ -215,20 +242,28 @@
             kv_copy(RELAY_Y, S4, part, y_down, sent_as=RELAY_Y).start()
 
     first_pair(S2)
-    for slot in (S1, S16):
-        arrived(slot, 1)
-        if slot != S16:
-            arrived(slot, 0)
-        first_pair(slot)
-
-    @pl.when(y > 0)
+
+    @pl.when(core == 0)
+    def _():
+        arrived(S1, 0)
+        arrived(S1, 1)
+        first_pair(S1)
+
+    arrived(S16, 1)
+    first_pair(S16)
+    early = (core == 1) & (y > 0)
+
+    @pl.when(early)
     def _():
         second_pair(S2)
 
-    for slot in (S4, S32):
-        arrived(slot, 0)
-        arrived(slot, 1)
-        first_pair(slot)
+    arrived(S4, 0)
+    arrived(S4, 1)
+    first_pair(S4)
+    cut_copy(OWN, S32, (c, h), True).wait_recv()
+    cut_copy(OWN, S32, (c, h), False).wait_recv()
+    arrived(S32, 1)
+    first_pair(S32)
 
     def finish(pair):
         for g in range(heads):
@@ -285,11 +320,15 @@
     with scope("plain_right"):
         plain(0, list(range(half, np_)))
 
-    @pl.when(y == 0)
+    @pl.when(jnp.logical_not(early))
     def _():
         second_pair(S2)
 
-    for slot in (S1, S16, S4, S32):
+    @pl.when(core == 0)
+    def _():
+        second_pair(S1)
+
+    for slot in (S16, S4, S32):
         second_pair(slot)
 
     with scope("finish_1"):
@@ -318,18 +357,12 @@
             own_s[j] = low
             own_s[half + j] = high
 
-    def out_copy(piece):
-        return pltpu.make_async_copy(
-            out_s.at[piece], o_hbm.at[:, pl.ds(pl.multiple_of(piece * pw, pw), pw)], out_sem.at[piece]
-        )
-
     def final(piece):
         near_copy(0, piece).wait_recv()
         near_copy(1, piece).wait_recv()
-        out_s[piece] = (
+        o_ref[:, pl.ds(pl.multiple_of(piece * pw, pw), pw)] = (
             own_s[piece] + near_recv[0, piece].astype(jnp.float32) + near_recv[1, piece].astype(jnp.float32)
-        ).astype(out_s.dtype)
-        out_copy(piece).start()
+        ).astype(o_ref.dtype)
 
     with scope("final"):
         @pl.loop(0, half)
@@ -338,7 +371,7 @@
             final(half + j)
 
     for part in range(2):
-        for slot in (S2, S1, S8, S16, S32):
+        for slot in (S2, S1, S8, S16):
             kv_copy(OWN, slot, part, (c, h)).wait_send()
 
         @pl.when(y < 3)
@@ -349,6 +382,10 @@
         def _():
             kv_copy(OWN, RELAY_Y, part, (c, h)).wait_send()
     kv_copy(OWN, RELAY, 1, (c, h)).wait_send()
+    kv_copy(OWN, S32, 1, (c, h)).wait_send()
+    cut_copy(OWN, S32, (c, h), True).wait_send()
+    cut_copy(OWN, RELAY, (c, h), False).wait_send()
+    cut_copy(OWN, S32, (c, h), False).wait_send()
 
     @pl.loop(0, half)
     def _(j):
@@ -359,7 +396,6 @@
     def _(j):
         near_copy(0, j).wait_send()
         near_copy(1, j).wait_send()
-        out_copy(j).wait()
 
 
 def per_device(queries, key_block, value_block, block_valid, out_weight):
@@ -375,9 +411,9 @@
     any_spec = pl.BlockSpec(memory_space=pl.ANY)
     return pl.pallas_call(
         kernel,
-        out_shape=jax.ShapeDtypeStruct((chunk, d), bf16),
+        out_shape=pltpu.VMEM((chunk, d), bf16),
         in_specs=[pl.BlockSpec(memory_space=pltpu.SMEM)] + [any_spec] * 4,
-        out_specs=any_spec,
+        out_specs=pl.BlockSpec(memory_space=pltpu.VMEM),
         scratch_shapes=[
             pltpu.VMEM((rows, qcols), bf16),
             pltpu.VMEM((9, 2, rows, hd), bf16),
@@ -391,7 +427,6 @@
             pltpu.VMEM((rows, qcols), bf16),
             pltpu.VMEM((np_, chunk, pw), f32),
             pltpu.VMEM((np_, chunk, pw), bf16),
-            pltpu.VMEM((np_, chunk, pw), bf16),
             pltpu.VMEM((2, half, chunk, pw), bf16),
             pltpu.VMEM((2, np_, chunk, pw), bf16),
             pltpu.VMEM((2, np_, chunk, pw), bf16),
@@ -399,14 +434,15 @@
             pltpu.SemaphoreType.DMA,
             pltpu.SemaphoreType.DMA((9, 2)),
             pltpu.SemaphoreType.DMA((9, 2)),
+            pltpu.SemaphoreType.DMA((3,)),
+            pltpu.SemaphoreType.DMA((3,)),
             pltpu.SemaphoreType.DMA((2, half)),
             pltpu.SemaphoreType.DMA((2, half)),
             pltpu.SemaphoreType.DMA((2, np_)),
             pltpu.SemaphoreType.DMA((2, np_)),
-            pltpu.SemaphoreType.DMA((np_,)),
         ],
         compiler_params=pltpu.CompilerParams(
-            collective_id=0, has_side_effects=True, vmem_limit_bytes=67_043_328
+            collective_id=0, has_side_effects=True, vmem_limit_bytes=65_900_000
         ),
         name="attend_project",
     )(block_valid, queries, key_block, value_block, out_weight)

time: 62.9 us -> 61.5 us (0.978)
  local copies, waits for them, and re-layouts: 2.16 us -> 0.93 us
    unnamed x1, local copies, waits for them, and re-layouts: 2.16 us -> 0.93 us
where the time goes in v3:
time: 61.5 us; the launch traced here: 61.4 us
  Pallas kernels  60.4 us (98%)
  local copies, waits for them, and re-layouts  0.93 us (2%)
    pallas_call x1, Pallas kernels, per_device(): pl.pallas_call(kernel, out_shape=pltpu.VMEM((chunk, d), bf16), in_specs=[...  60.4 us

profile of v3, /device:TPU:8, one launch (start us, length us, event | category | flops | bytes accessed | tf_op | source)
XLA Modules:
  0.0 61.4 jit_solution(6852835235031120328)
XLA Ops:
  0.0 60.4 %attend_project.1 = bf16[128,3584]{1,0:T(8,128)(2,1)S(1)} custom-call(s32[64]{0:T(128)} %valid_ref.1, bf16[512,896]{1,0:T(8,128)(2,1)} %q_hbm.1, bf16[512,128]{1,0:T(8,128)(2,1)} %k_hbm.1, bf16[512,128]{1,0:T(8,128)(2,1)} %v_hbm.1, bf16[896,3584]{1,0:T(8,128)(2,1)} %w_hbm.1), custom_call_target="tpu_custom_call" | custom-call | tf_op jit(solution)/shard_map/attend_project/pallas_call | solution.py:412
  60.4 0.9 %copy.7 = bf16[128,3584]{1,0:T(8,128)(2,1)} copy(bf16[128,3584]{1,0:T(8,128)(2,1)S(1)} %attend_project.1) | data formatting | bytes 1835008

commit v4 on v3

--- a/solution.py
+++ b/solution.py
@@ -211,19 +211,21 @@
 
     pass_on_s8(1)
 
-    def pass_on_s2():
-        for part in range(2):
-            arrived(S2, part)
-
-            @pl.when(core == 1)
-            def _():
-                kv_copy(S2, S1, part, other).start()
-
-            @pl.when(y < 3)
-            def _():
-                kv_copy(S2, S4, part, y_up).start()
-
-    pl.when(y > 0)(pass_on_s2)
+    def pass_on_s2(part):
+        arrived(S2, part)
+
+        @pl.when(core == 1)
+        def _():
+            kv_copy(S2, S1, part, other).start()
+
+        @pl.when(y < 3)
+        def _():
+            kv_copy(S2, S4, part, y_up).start()
+
+    @pl.when(y > 0)
+    def _():
+        pass_on_s2(0)
+        pass_on_s2(1)
 
     @pl.when(c >= OFFSETS[S8])
     def _():
@@ -231,39 +233,58 @@
             set_vt(S8)
             tiles(S8, 0, 2 * heads)
 
+    @pl.when(y > 0)
+    def _():
+        first_pair(S2)
+
     arrived(S16, 0)
     cut_copy(S16, S32, z_up2, True).start()
-    pl.when(y == 0)(pass_on_s2)
-
-    @pl.when(y == 1)
-    def _():
-        for part in range(2):
+
+    def relay_y(part):
+        @pl.when(y == 1)
+        def _():
             arrived(RELAY_Y, part)
             kv_copy(RELAY_Y, S4, part, y_down, sent_as=RELAY_Y).start()
 
-    first_pair(S2)
-
-    @pl.when(core == 0)
-    def _():
+    def first_s1():
         arrived(S1, 0)
         arrived(S1, 1)
         first_pair(S1)
 
+    relay_y(0)
+
+    @pl.when(y == 0)
+    def _():
+        pass_on_s2(0)
+
+    pl.when((core == 0) & (y > 0))(first_s1)
     arrived(S16, 1)
+    relay_y(1)
     first_pair(S16)
+
+    @pl.when(y == 0)
+    def _():
+        pass_on_s2(1)
+        first_pair(S2)
+
+    pl.when((core == 0) & (y == 0))(first_s1)
     early = (core == 1) & (y > 0)
 
     @pl.when(early)
     def _():
         second_pair(S2)
 
-    arrived(S4, 0)
-    arrived(S4, 1)
-    first_pair(S4)
+    def first_s4():
+        arrived(S4, 0)
+        arrived(S4, 1)
+        first_pair(S4)
+
+    pl.when(y != 1)(first_s4)
     cut_copy(OWN, S32, (c, h), True).wait_recv()
     cut_copy(OWN, S32, (c, h), False).wait_recv()
     arrived(S32, 1)
     first_pair(S32)
+    pl.when(y == 1)(first_s4)
 
     def finish(pair):
         for g in range(heads):

time: 61.5 us -> 61.9 us (level); the launches traced: 61.4 us -> 60.8 us
  no operation moved by 1% of the time
where the time goes in v4:
time: 61.9 us; the launch traced here: 60.8 us
  Pallas kernels  59.8 us (97%)
  local copies, waits for them, and re-layouts  0.93 us (2%)
    pallas_call x1, Pallas kernels, per_device(): pl.pallas_call(kernel, out_shape=pltpu.VMEM((chunk, d), bf16), in_specs=[...  59.8 us

profile of v4, /device:TPU:8, one launch (start us, length us, event | category | flops | bytes accessed | tf_op | source)
XLA Modules:
  0.0 60.8 jit_solution(15313672967966131170)
XLA Ops:
  0.0 59.8 %attend_project.1 = bf16[128,3584]{1,0:T(8,128)(2,1)S(1)} custom-call(s32[64]{0:T(128)} %valid_ref.1, bf16[512,896]{1,0:T(8,128)(2,1)} %q_hbm.1, bf16[512,128]{1,0:T(8,128)(2,1)} %k_hbm.1, bf16[512,128]{1,0:T(8,128)(2,1)} %v_hbm.1, bf16[896,3584]{1,0:T(8,128)(2,1)} %w_hbm.1), custom_call_target="tpu_custom_call" | custom-call | tf_op jit(solution)/shard_map/attend_project/pallas_call | solution.py:433
  59.8 0.9 %copy.7 = bf16[128,3584]{1,0:T(8,128)(2,1)} copy(bf16[128,3584]{1,0:T(8,128)(2,1)S(1)} %attend_project.1) | data formatting | bytes 1835008

commit v5 on v4

--- a/solution.py
+++ b/solution.py
@@ -258,7 +258,11 @@
         pass_on_s2(0)
 
     pl.when((core == 0) & (y > 0))(first_s1)
-    arrived(S16, 1)
+
+    @pl.when(c >= OFFSETS[S16])
+    def _():
+        arrived(S16, 1)
+
     relay_y(1)
     first_pair(S16)
 
@@ -279,12 +283,15 @@
         arrived(S4, 1)
         first_pair(S4)
 
-    pl.when(y != 1)(first_s4)
-    cut_copy(OWN, S32, (c, h), True).wait_recv()
-    cut_copy(OWN, S32, (c, h), False).wait_recv()
-    arrived(S32, 1)
+    def wait_s32():
+        cut_copy(OWN, S32, (c, h), True).wait_recv()
+        cut_copy(OWN, S32, (c, h), False).wait_recv()
+        arrived(S32, 1)
+
+    pl.when(y > 1)(first_s4)
+    pl.when(c >= OFFSETS[S32])(wait_s32)
     first_pair(S32)
-    pl.when(y == 1)(first_s4)
+    pl.when(y <= 1)(first_s4)
 
     def finish(pair):
         for g in range(heads):
@@ -390,6 +397,12 @@
         def _(j):
             final(j)
             final(half + j)
+
+    pl.when(c < OFFSETS[S32])(wait_s32)
+
+    @pl.when(c < OFFSETS[S16])
+    def _():
+        arrived(S16, 1)
 
     for part in range(2):
         for slot in (S2, S1, S8, S16):

time: 61.9 us -> 60.8 us (0.982)
    pallas_call x1, Pallas kernels: 59.8 us -> 59.2 us  [per_device(): pl.pallas_call(kernel, out_shape=pltpu.VMEM((chunk, d), bf16), in_specs=[...]
where the time goes in v5:
time: 60.8 us; the launch traced here: 60.1 us
  Pallas kernels  59.2 us (97%)
  local copies, waits for them, and re-layouts  0.93 us (2%)
    pallas_call x1, Pallas kernels, per_device(): pl.pallas_call(kernel, out_shape=pltpu.VMEM((chunk, d), bf16), in_specs=[...  59.2 us

profile of v5, /device:TPU:8, one launch (start us, length us, event | category | flops | bytes accessed | tf_op | source)
XLA Modules:
  0.0 60.1 jit_solution(16542755097499606756)
XLA Ops:
  0.0 59.2 %attend_project.1 = bf16[128,3584]{1,0:T(8,128)(2,1)S(1)} custom-call(s32[64]{0:T(128)} %valid_ref.1, bf16[512,896]{1,0:T(8,128)(2,1)} %q_hbm.1, bf16[512,128]{1,0:T(8,128)(2,1)} %k_hbm.1, bf16[512,128]{1,0:T(8,128)(2,1)} %v_hbm.1, bf16[896,3584]{1,0:T(8,128)(2,1)} %w_hbm.1), custom_call_target="tpu_custom_call" | custom-call | tf_op jit(solution)/shard_map/attend_project/pallas_call | solution.py:446
  59.2 0.9 %copy.7 = bf16[128,3584]{1,0:T(8,128)(2,1)} copy(bf16[128,3584]{1,0:T(8,128)(2,1)S(1)} %attend_project.1) | data formatting | bytes 1835008
